TPU v7x, 32 devices: a whole 2x2x4 slice. The times are simulated.
32 devices in a mesh: dp: 8 (over y, x, core), own: 4 (over z).
Axes of the slice: x: 2, y: 2, z: 4, core: 2. Of those that a mesh axis runs over, the one named last changes fastest.
Arguments:
- grad: bfloat16 [8192, 1024], P(('dp', 'own')), may hold values from -88 to 88
- left_stats: float32 [8, 1024, 1024], P('dp', 'own'), may hold values from -0.4 to 2.6
- right_stats: float32 [8, 1024, 1024], P('dp', 'own'), may hold values from -0.4 to 2.6
- left_roots: float32 [8, 1024, 1024], P('dp', 'own'), may hold values from -0.4 to 2.6, as said below
- right_roots: float32 [8, 1024, 1024], P('dp', 'own'), may hold values from -0.4 to 2.6, as said below
Outputs:
- direction: bfloat16 [8192, 1024], P(('dp', 'own'))
- left_new: float32 [8, 1024, 1024], P('dp', 'own')
- right_new: float32 [8, 1024, 1024], P('dp', 'own')
Inputs may be any that keep to these rules, and one draw needn't show every extreme that they name: `right_roots`: each block's feature-side root is symmetric. `left_roots`: each block's vocabulary-side root is symmetric.
All inputs are finite; a program needn't handle non-finite values.
Results may differ from a plain program's by a relative error of at most 0.0049.
Values may be sent and summed in bfloat16 or wider, within the bound.
No kernel may reach another device: no remote copies, remote signals or barrier semaphores. Data moves between devices by JAX's collectives and lax.ppermute only.
A program may use at most 64 MiB of HBM per device.

v0:
```python
import jax
import jax.numpy as jnp
from jax import lax
from jax.sharding import PartitionSpec as P

highest = lax.Precision.HIGHEST
epsilon = 1e-06


def transpose_product(left_side, right_side):
    return lax.dot_general(
        left_side, right_side, (((0,), (0,)), ((), ())), preferred_element_type=jnp.float32
    )


def local(grad, left_stats, right_stats, left_roots, right_roots):
    feature_width = grad.shape[1]
    owner_count = lax.axis_size("own")
    slice_width = feature_width // owner_count
    own_rows = grad.astype(jnp.float32)
    grad_square = jnp.sum(own_rows * own_rows)
    whole_grad = lax.all_gather(grad, "own", axis=0, tiled=True)
    feature_cols = lax.dynamic_slice_in_dim(
        whole_grad, lax.axis_index("own") * slice_width, slice_width, 1
    )
    left_gram = lax.dot_general(
        grad, whole_grad, (((1,), (1,)), ((), ())), preferred_element_type=jnp.float32
    )
    right_gram = transpose_product(feature_cols, whole_grad)
    left_update = 0.9 * left_stats[0] + 0.1 / feature_width * left_gram
    right_update = 0.9 * right_stats[0] + 0.1 / feature_width * right_gram
    mixed_cols = lax.dot_general(
        whole_grad.astype(jnp.float32), right_roots[0], (((1,), (1,)), ((), ())), precision=highest
    )
    mixed_cols = mixed_cols.astype(jnp.bfloat16)
    precond = jnp.dot(
        left_roots[0],
        lax.all_gather(mixed_cols, "own", axis=1, tiled=True).astype(jnp.float32),
        precision=highest,
    )
    precond_square = jnp.sum(precond * precond)
    norm_totals = lax.psum((grad_square, precond_square), "own")
    graft_scale = jnp.sqrt(norm_totals[0] / (norm_totals[1] + epsilon))
    direction = (precond * graft_scale).astype(jnp.bfloat16)
    return (direction, left_update[None], right_update[None])


def solution(mesh):
    in_specs = (
        P(("dp", "own"), None),
        P("dp", "own", None),
        P("dp", "own", None),
        P("dp", "own", None),
        P("dp", "own", None),
    )
    out_specs = (P(("dp", "own"), None), P("dp", "own", None), P("dp", "own", None))
    return jax.shard_map(local, mesh=mesh, in_specs=in_specs, out_specs=out_specs, check_vma=False)
```

profile of v0, /device:TPU:0, one launch (start us, length us, event | category | flops | bytes accessed | tf_op | source)
XLA Modules:
  0.0 131.7 jit_solution(18139367668326251888)
XLA Ops:
  7.2 0.0 copy-start
  7.2 0.0 all-gather.3.cloned.1.call-start
  7.2 0.7 all-gather.3.cloned.1.call-update
  7.9 0.0 all-gather.5.cloned.1.call-start
  8.0 50.0 %all-gather.3.cloned.1.call-done = bf16[1024,1024]{1,0:T(8,128)(2,1)} async-done(((bf16[256,1024]{1,0:T(8,128)(2,1)}), bf16[1024,1024]{1,0:T(8,128)(2,1)}) %all-gather.3.cloned.1.call-update) | async-done | bytes 2097168 | tf_op jit(solution)/shard_map/all_gather | solution.py:22
  58.0 0.0 copy-start.1
  58.0 4.7 %convolution_convert_fusion = bf16[1024,256]{1,0:T(8,128)(2,1)} fusion(bf16[1024,1024]{1,0:T(8,128)(2,1)} %all-gather.3.cloned.1.call-done, f32[1,256,1024]{2,1,0:T(8,128)} %param.9), kind=kOutput, calls=%fused_computation.6 | convolution fusion | flops 3221487616 | bytes 3670016 | tf_op jit(solution)/shard_map/dot_general | solution.py:32
  62.6 0.0 all-gather.5.cloned.1.call-update
  62.7 1.9 %multiply_reduce_fusion.1 = f32[]{:T(128)} fusion(bf16[256,1024]{1,0:T(8,128)(2,1)} %param.5), kind=kLoop, calls=%fused_computation.12 | loop fusion | flops 786431 | bytes 524292 | tf_op jit(solution)/shard_map/reduce_sum | solution.py:21
  64.6 0.0 copy-done.1
  64.6 0.0 copy-start.2
  64.6 0.0 copy-start.3
  64.6 3.1 %fusion.1 = f32[1,256,1024]{2,1,0:T(8,128)} fusion(bf16[1024,1024]{1,0:T(8,128)(2,1)S(1)} %copy-done.1, f32[1,256,1024]{2,1,0:T(8,128)} %param.7, s32[]{:T(128)S(6)} %select_n.3), kind=kOutput, calls=%fused_computation.2 | convolution fusion | flops 537657344 | bytes 4718596 | tf_op jit(solution)/shard_map/dot_general | solution.py:11
  67.7 0.0 copy-done.2
  67.7 0.0 copy-done.3
  67.7 1.8 %fusion.3 = f32[1,256,1024]{2,1,0:T(8,128)} fusion(bf16[256,1024]{1,0:T(8,128)(2,1)S(1)} %copy-done.2, bf16[1024,1024]{1,0:T(8,128)(2,1)S(1)} %copy-done.1, f32[1,256,1024]{2,1,0:T(8,128)S(1)} %copy-done.3), kind=kOutput, calls=%fused_computation.5 | convolution fusion | flops 537657344 | bytes 4718592 | tf_op jit(solution)/shard_map/dot_general | solution.py:26
  69.4 38.4 %all-gather.5.cloned.1.call-done = bf16[1024,1024]{1,0:T(8,128)(2,1)} async-done(((bf16[1024,256]{1,0:T(8,128)(2,1)}), bf16[1024,1024]{1,0:T(8,128)(2,1)}) %all-gather.5.cloned.1.call-update) | async-done | bytes 2097168 | tf_op jit(solution)/shard_map/all_gather | solution.py:38
  107.9 0.0 copy-done
  107.9 4.6 %multiply_reduce_fusion = (f32[]{:T(128)}, f32[1024,256]{1,0:T(8,128)S(1)}) fusion(bf16[1024,1024]{1,0:T(8,128)(2,1)} %all-gather.5.cloned.1.call-done, f32[1,256,1024]{2,1,0:T(8,128)S(1)} %copy-done), kind=kOutput, calls=%fused_computation.11 | convolution fusion | flops 3221749760 | bytes 4194308 | tf_op jit(solution)/shard_map/dot_general | solution.py:36
  112.4 10.0 %all-reduce = (f32[]{:T(128)}, f32[]{:T(128)}) all-reduce(f32[]{:T(128)} %multiply_reduce_fusion.1, f32[]{:T(128)} %get-tuple-element.8), channel_id=1, replica_groups=mesh['dp'=8,'own'=4] {'own'}, use_global_device_ids=true, to_apply=%region_1.0 | all-reduce | flops 2 | bytes 16 | tf_op jit(solution)/shard_map/psum | solution.py:42
  123.7 0.1 fusion.7
  123.9 1.0 copy.8
Async XLA Ops:
  7.2 100.7 %copy-start = (f32[1,256,1024]{2,1,0:T(8,128)S(1)}, f32[1,256,1024]{2,1,0:T(8,128)}, u32[]{:S(2)}) copy-start(f32[1,256,1024]{2,1,0:T(8,128)} %param.8) | copy-start | bytes 3145732
  7.2 50.8 %all-gather.3.cloned.1.call-start = ((), (), s32[]{:S(2)}) async-start(), calls=%async_computation | async-start | bytes 2621440 | tf_op jit(solution)/shard_map/all_gather | solution.py:22
  7.9 100.0 %all-gather.5.cloned.1.call-start = ((), (), s32[]{:S(2)}) async-start(), calls=%async_computation.1 | async-start | bytes 2621440 | tf_op jit(solution)/shard_map/all_gather | solution.py:38
  58.0 6.6 %copy-start.1 = (bf16[1024,1024]{1,0:T(8,128)(2,1)S(1)}, bf16[1024,1024]{1,0:T(8,128)(2,1)}, u32[]{:S(2)}) copy-start(bf16[1024,1024]{1,0:T(8,128)(2,1)} %all-gather.3.cloned.1.call-done) | copy-start | bytes 6291460
  64.6 3.1 %copy-start.2 = (bf16[256,1024]{1,0:T(8,128)(2,1)S(1)}, bf16[256,1024]{1,0:T(8,128)(2,1)}, u32[]{:S(2)}) copy-start(bf16[256,1024]{1,0:T(8,128)(2,1)} %param.5) | copy-start | bytes 1572868
  64.6 3.1 %copy-start.3 = (f32[1,256,1024]{2,1,0:T(8,128)S(1)}, f32[1,256,1024]{2,1,0:T(8,128)}, u32[]{:S(2)}) copy-start(f32[1,256,1024]{2,1,0:T(8,128)} %param.6) | copy-start | bytes 3145732
Sparse Core Ops, SparseCore 0:
  9.6 48.3 all-gather.2
  62.8 45.0 all-gather.4
where the time goes:
time: 132 us
  waiting for transfers between devices  89.2 us (68%)
  between operations  15.3 us (12%)
  matrix products  14.1 us (11%)
  blocking collectives  10 us (8%)
  other arithmetic  2.01 us (2%)
    all_gather x1, waiting for transfers between devices, local(): whole_grad = lax.all_gather(grad, 'own', axis=0, tiled=True)  50 us
    all_gather x1, waiting for transfers between devices, local(): lax.all_gather(mixed_cols, 'own', axis=1, tiled=True).astype(jnp.float32)  38.4 us
    psum x1, blocking collectives, local(): norm_totals = lax.psum((grad_square, precond_square), 'own')  10 us
    dot_general x1, matrix products, local(): lax.dot_general(whole_grad.astype(jnp.float32), right_roots[0], (((1,), (...  4.66 us
    dot_general x1, matrix products, local(): jnp.dot(left_roots[0], lax.all_gather(mixed_cols, 'own', axis=1, tiled=Tr...  4.57 us
    dot_general x1, matrix products, transpose_product(): lax.dot_general(left_side, right_side, (((0,), (0,)), ((), ())), preferre...  3.07 us
  transfers between devices with their start and end apart: 2, of which 2 were waited for; matrix products, arithmetic and copies ran while one was open for 5% of the time, Pallas kernels for 0%

commit v1 on v0

--- a/solution.py
+++ b/solution.py
@@ -19,7 +19,12 @@
     slice_width = feature_width // owner_count
     own_rows = grad.astype(jnp.float32)
     grad_square = jnp.sum(own_rows * own_rows)
-    whole_grad = lax.all_gather(grad, "own", axis=0, tiled=True)
+    ring = [grad]
+    for hop in range(3):
+        ring.append(lax.ppermute(ring[-1], "own", [(dev, (dev + 1) % 4) for dev in range(4)]))
+    whole_grad = jnp.roll(
+        jnp.concatenate(ring[::-1], axis=0), (lax.axis_index("own") + 1) * ring[0].shape[0], axis=0
+    )
     feature_cols = lax.dynamic_slice_in_dim(
         whole_grad, lax.axis_index("own") * slice_width, slice_width, 1
     )

time: 132 us -> 128 us (0.970)
  waiting for transfers between devices: 89.2 us -> 71.7 us
  local copies, waits for them, and re-layouts: 1.02 us -> 12.2 us
  starting transfers between devices: 0.08 us -> 3.15 us
    all_gather x1 -> x0, waiting for transfers between devices: 50 us -> none  [local(): whole_grad = lax.all_gather(grad, 'own', axis=0, tiled=True)]
    ppermute x0 -> x3, waiting for transfers between devices: none -> 43.1 us  [local(): lax.ppermute(ring[-1], 'own', [(dev, (dev + 1) % 4) for dev in range(4)])]
    unnamed x9 -> x20, local copies, waits for them, and re-layouts: 1.02 us -> 12.2 us
    all_gather x1, waiting for transfers between devices: 38.4 us -> 28.7 us  [local(): lax.all_gather(mixed_cols, 'own', axis=1, tiled=True).astype(jnp.float32)]
    ppermute x0 -> x3, starting transfers between devices: none -> 3.11 us  [local(): lax.ppermute(ring[-1], 'own', [(dev, (dev + 1) % 4) for dev in range(4)])]
    dot_general x1, matrix products: 4.66 us -> 2.66 us  [local(): lax.dot_general(whole_grad.astype(jnp.float32), right_roots[0], (((1,), (...]
    dot_general x1, matrix products: 1.77 us -> 3.37 us  [local(): lax.dot_general(grad, whole_grad, (((1,), (1,)), ((), ())), preferred_ele...]
  transfers between devices with their start and end apart: 2 -> 4, of which waited for: 2 -> 4; matrix products, arithmetic and copies ran while one was open for 5% -> 12% of each run, Pallas kernels for 0% -> 0%
where the time goes in v1:
time: 128 us
  waiting for transfers between devices  71.7 us (56%)
  between operations  15.5 us (12%)
  matrix products  13.8 us (11%)
  local copies, waits for them, and re-layouts  12.2 us (10%)
  blocking collectives  10.1 us (8%)
  starting transfers between devices  3.15 us (2%)
    ppermute x3, waiting for transfers between devices, local(): lax.ppermute(ring[-1], 'own', [(dev, (dev + 1) % 4) for dev in range(4)])  43.1 us
    all_gather x1, waiting for transfers between devices, local(): lax.all_gather(mixed_cols, 'own', axis=1, tiled=True).astype(jnp.float32)  28.7 us
    unnamed x20, local copies, waits for them, and re-layouts  12.2 us
    psum x1, blocking collectives, local(): norm_totals = lax.psum((grad_square, precond_square), 'own')  10.1 us
    dot_general x1, matrix products, local(): jnp.dot(left_roots[0], lax.all_gather(mixed_cols, 'own', axis=1, tiled=Tr...  4.56 us
    dot_general x1, matrix products, local(): lax.dot_general(grad, whole_grad, (((1,), (1,)), ((), ())), preferred_ele...  3.37 us
    dot_general x1, matrix products, transpose_product(): lax.dot_general(left_side, right_side, (((0,), (0,)), ((), ())), preferre...  3.24 us
    ppermute x3, starting transfers between devices, local(): lax.ppermute(ring[-1], 'own', [(dev, (dev + 1) % 4) for dev in range(4)])  3.11 us
  transfers between devices with their start and end apart: 4, of which 4 were waited for; matrix products, arithmetic and copies ran while one was open for 12% of the time, Pallas kernels for 0%

profile of v1, /device:TPU:0, one launch (start us, length us, event | category | flops | bytes accessed | tf_op | source)
XLA Modules:
  0.0 127.6 jit_solution(6366069081329751119)
XLA Ops:
  7.2 0.0 copy-start
  7.2 0.0 copy-start.2
  7.2 0.0 all-gather.2.cloned.1.call-start
  7.2 3.1 %collective-permute-start = (bf16[256,1024]{1,0:T(8,128)(2,1)}, bf16[256,1024]{1,0:T(8,128)(2,1)S(1)}, u32[]{:S(2)}, u32[]{:S(2)}) collective-permute-start(bf16[256,1024]{1,0:T(8,128)(2,1)} %param.5), channel_id=1, source_target_pairs={{0,1},{1,2},{2,3},{3,0},{4,5},{5,6},{6,7},{7,4},{8,9},{9,10},{10,1... | collective-permute-start | bytes 1572872 | tf_op jit(solution)/shard_map/ppermute | solution.py:24
  10.3 14.2 %collective-permute-done = bf16[256,1024]{1,0:T(8,128)(2,1)S(1)} collective-permute-done((bf16[256,1024]{1,0:T(8,128)(2,1)}, bf16[256,1024]{1,0:T(8,128)(2,1)S(1)}, u32[]{:S(2)}, u32[]{:S(2)}) %collective-permute-start) | collective-permute-done | bytes 524320 | tf_op jit(solution)/shard_map/ppermute | solution.py:24
  24.5 0.0 collective-permute-start.1
  24.5 14.9 %collective-permute-done.1 = bf16[256,1024]{1,0:T(8,128)(2,1)S(1)} collective-permute-done((bf16[256,1024]{1,0:T(8,128)(2,1)S(1)}, bf16[256,1024]{1,0:T(8,128)(2,1)S(1)}, u32[]{:S(2)}, u32[]{:S(2)}) %collective-permute-start.1) | collective-permute-done | bytes 524320 | tf_op jit(solution)/shard_map/ppermute | solution.py:24
  39.4 14.0 %collective-permute-done.2 = bf16[256,1024]{1,0:T(8,128)(2,1)S(1)} collective-permute-done((bf16[256,1024]{1,0:T(8,128)(2,1)S(1)}, bf16[256,1024]{1,0:T(8,128)(2,1)S(1)}, u32[]{:S(2)}, u32[]{:S(2)}) %collective-permute-start.2) | collective-permute-done | bytes 524320 | tf_op jit(solution)/shard_map/ppermute | solution.py:24
  53.5 1.1 constant_dynamic-update-slice_fusion.4
  54.8 1.9 %copy-done.1 = bf16[2048,1024]{1,0:T(8,128)(2,1)} copy-done((bf16[2048,1024]{1,0:T(8,128)(2,1)}, bf16[2048,1024]{1,0:T(8,128)(2,1)S(1)}, u32[]{:S(2)}) %copy-start.1) | copy-done | bytes 4194328
  56.8 2.7 %fusion.27 = bf16[1024,256]{1,0:T(8,128)(2,1)} fusion(bf16[2048,1024]{1,0:T(8,128)(2,1)S(1)} %constant_dynamic-update-slice_fusion, s32[]{:T(128)S(6)} %select_n.21, f32[1,256,1024]{2,1,0:T(8,128)S(1)} %copy-done.3), kind=kOutput, calls=%fused_computation.13 | convolution fusion | flops 3221487616 | bytes 3670020 | tf_op jit(solution)/shard_map/dot_general | solution.py:37
  59.4 0.0 all-gather.2.cloned.1.call-update
  59.5 1.6 %copy.8 = f32[1,256,1024]{1,2,0:T(8,128)S(1)} copy(f32[1,256,1024]{2,1,0:T(8,128)} %param.6) | data formatting | bytes 2097152 | tf_op args[1]
  61.0 2.6 %copy.9 = f32[1,256,1024]{1,2,0:T(8,128)} copy(f32[1,256,1024]{2,1,0:T(8,128)} %param.7) | data formatting | bytes 2097152 | tf_op args[2]
  63.6 0.9 multiply_reduce_fusion.1
  64.5 3.4 %fusion.15 = f32[1,256,1024]{1,2,0:T(8,128)} fusion(bf16[256,1024]{1,0:T(8,128)(2,1)S(1)} %copy-done.2, bf16[2048,1024]{1,0:T(8,128)(2,1)} %copy-done.1, s32[]{:T(128)S(6)} %select_n.21, f32[1,256,1024]{1,2,0:T(8,128)S(1)} %copy.8), kind=kOutput, calls=%fused_computation.9 | convolution fusion | flops 537657344 | bytes 4718596 | tf_op jit(solution)/shard_map/dot_general | solution.py:31
  67.9 2.5 %copy.12 = f32[1,256,1024]{2,1,0:T(8,128)} copy(f32[1,256,1024]{1,2,0:T(8,128)} %fusion.15) | data formatting | bytes 2097152
  70.4 3.2 %fusion.24 = f32[1,256,1024]{1,2,0:T(8,128)S(1)} fusion(bf16[2048,1024]{1,0:T(8,128)(2,1)} %copy-done.1, s32[]{:T(128)S(6)} %select_n.21, f32[1,256,1024]{1,2,0:T(8,128)} %copy.9, s32[]{:T(128)S(6)} %select_n.22, s32[]{:T(128)S(6)} %select_n.24), kind=kOutput, calls=%fused_computation.12 | convolution fusion | flops 537657344 | bytes 4718604 | tf_op jit(solution)/shard_map/dot_general | solution.py:11
  73.7 1.3 %copy.13 = f32[1,256,1024]{2,1,0:T(8,128)} copy(f32[1,256,1024]{1,2,0:T(8,128)S(1)} %fusion.24) | data formatting | bytes 2097152
  75.0 28.7 %all-gather.2.cloned.1.call-done = bf16[1024,1024]{1,0:T(8,128)(2,1)} async-done(((bf16[1024,256]{1,0:T(8,128)(2,1)}), bf16[1024,1024]{1,0:T(8,128)(2,1)}) %all-gather.2.cloned.1.call-update) | async-done | bytes 2097168 | tf_op jit(solution)/shard_map/all_gather | solution.py:43
  103.6 4.6 %multiply_reduce_fusion = (f32[]{:T(128)}, f32[1024,256]{1,0:T(8,128)S(1)}) fusion(bf16[1024,1024]{1,0:T(8,128)(2,1)} %all-gather.2.cloned.1.call-done, f32[1,256,1024]{2,1,0:T(8,128)S(1)} %copy-done), kind=kOutput, calls=%fused_computation.18 | convolution fusion | flops 3221749760 | bytes 4194308 | tf_op jit(solution)/shard_map/dot_general | solution.py:41
  108.2 10.1 %all-reduce = (f32[]{:T(128)}, f32[]{:T(128)}) all-reduce(f32[]{:T(128)} %multiply_reduce_fusion.1, f32[]{:T(128)} %get-tuple-element.8), channel_id=1, replica_groups=mesh['dp'=8,'own'=4] {'own'}, use_global_device_ids=true, to_apply=%region_1.2 | all-reduce | flops 2 | bytes 16 | tf_op jit(solution)/shard_map/psum | solution.py:47
  119.7 0.1 fusion.33
  119.8 1.0 copy.11
  (13 shorter events, 0.3 us)
Async XLA Ops:
  7.2 96.5 %copy-start = (f32[1,256,1024]{2,1,0:T(8,128)S(1)}, f32[1,256,1024]{2,1,0:T(8,128)}, u32[]{:S(2)}) copy-start(f32[1,256,1024]{2,1,0:T(8,128)} %param.8) | copy-start | bytes 3145732
  7.2 47.6 %copy-start.2 = (bf16[256,1024]{1,0:T(8,128)(2,1)S(1)}, bf16[256,1024]{1,0:T(8,128)(2,1)}, u32[]{:S(2)}) copy-start(bf16[256,1024]{1,0:T(8,128)(2,1)} %param.5) | copy-start | bytes 1572868
  7.2 96.4 %all-gather.2.cloned.1.call-start = ((), (), s32[]{:S(2)}) async-start(), calls=%async_computation | async-start | bytes 2621440 | tf_op jit(solution)/shard_map/all_gather | solution.py:43
  7.2 17.3 %collective-permute-start = (bf16[256,1024]{1,0:T(8,128)(2,1)}, bf16[256,1024]{1,0:T(8,128)(2,1)S(1)}, u32[]{:S(2)}, u32[]{:S(2)}) collective-permute-start(bf16[256,1024]{1,0:T(8,128)(2,1)} %param.5), channel_id=1, source_target_pairs={{0,1},{1,2},{2,3},{3,0},{4,5},{5,6},{6,7},{7,4},{8,9},{9,10},{10,1... | collective-permute-start | bytes 1572872 | tf_op jit(solution)/shard_map/ppermute | solution.py:24
  24.5 14.9 %collective-permute-start.1 = (bf16[256,1024]{1,0:T(8,128)(2,1)S(1)}, bf16[256,1024]{1,0:T(8,128)(2,1)S(1)}, u32[]{:S(2)}, u32[]{:S(2)}) collective-permute-start(bf16[256,1024]{1,0:T(8,128)(2,1)S(1)} %collective-permute-done), channel_id=1, source_target_pairs={{0,1},{1,2},{2,3},{3,0},{4,5},{5,6},{6,7},{7,4},{8,9},{9,10},{10,1... | collective-permute-start | bytes 1572872 | tf_op jit(solution)/shard_map/ppermute | solution.py:24
  39.4 14.0 %collective-permute-start.2 = (bf16[256,1024]{1,0:T(8,128)(2,1)S(1)}, bf16[256,1024]{1,0:T(8,128)(2,1)S(1)}, u32[]{:S(2)}, u32[]{:S(2)}) collective-permute-start(bf16[256,1024]{1,0:T(8,128)(2,1)S(1)} %collective-permute-done.1), channel_id=1, source_target_pairs={{0,1},{1,2},{2,3},{3,0},{4,5},{5,6},{6,7},{7,4},{8,9},{9,10},{10,1... | collective-permute-start | bytes 1572872 | tf_op jit(solution)/shard_map/ppermute | solution.py:24
  39.4 17.4 %copy-start.3 = (f32[1,256,1024]{2,1,0:T(8,128)S(1)}, f32[1,256,1024]{2,1,0:T(8,128)}, u32[]{:S(2)}) copy-start(f32[1,256,1024]{2,1,0:T(8,128)} %param.9) | copy-start | bytes 3145732
  54.8 1.9 %copy-start.1 = (bf16[2048,1024]{1,0:T(8,128)(2,1)}, bf16[2048,1024]{1,0:T(8,128)(2,1)S(1)}, u32[]{:S(2)}) copy-start(bf16[2048,1024]{1,0:T(8,128)(2,1)S(1)} %constant_dynamic-update-slice_fusion) | copy-start | bytes 12582916
Sparse Core Ops, SparseCore 0:
  59.6 44.0 all-gather.1
